TPU v7x, 512 devices: a whole 4x8x8 slice. The times are simulated.
512 devices in a mesh: gx: 4 (over x), gy: 8 (over z), gz: 16 (over y, core).
Axes of the slice: x: 4, y: 8, z: 8, core: 2. Of those that a mesh axis runs over, the one named last changes fastest.
Arguments:
- positions: float32 [3, 262144], P(None, ('gx', 'gy', 'gz')), may hold values from -6 to 6
- frames: float32 [128, 3, 4096], P(None, None, ('gy', 'gz')), may hold values from -6 to 6
- path_slot: int32 [512, 32], P(('gx', 'gy', 'gz')), may hold values from 0 to 511, as said below
- path_count: int32 [512], replicated, may hold values from 1 to 32, 4096 in all
- path_order: int32 [4096], replicated, may hold values from 0 to 4095, each once
- frame_rank: int32 [128], replicated, may hold values from 0 to 127, each once
Outputs:
- forces: float32 [3, 262144], P(None, ('gx', 'gy', 'gz'))
- path_cv: float32 [2], replicated
Inputs may be any that keep to these rules, and one draw needn't show every extreme that they name: `path_slot`: within one domain's row the 32 local atom indices are all different.
All inputs are finite; a program needn't handle non-finite values.
Results may differ from a plain program's by a relative error of at most 0.00013.
Values sent between devices are 32-bit elements; how exact they have to be, the bound alone decides.
No kernel may reach another device: no remote copies, remote signals or barrier semaphores. Data moves between devices by JAX's collectives and lax.ppermute only.
A program may use at most 64 MiB of HBM per device.

v0:
```python
import jax
import jax.numpy as jnp
from jax import lax
from jax.sharding import Mesh
from jax.sharding import PartitionSpec as P

P_SIZE = 4096
GX_GY_GZ = ("gx", "gy", "gz_0", "gz_1")
GY_GZ = ("gy", "gz_0", "gz_1")
STRENGTH = 20.0
S_HOME = 0.5
KAPPA_S = 0.5
KAPPA_Z = 0.05
PAIR_SCALE = 0.02
WIDTH_SQ = 4.0


def one_axis_at_a_time(array, axes):
    for axis in axes:
        array = lax.psum(array, axis)
    return array


def pair_block(block_pos, all_pos):
    diff = block_pos[:, :, None] - all_pos[:, None, :]
    dist_sq = jnp.sum(diff * diff, axis=0)
    weight = PAIR_SCALE * jnp.exp(-dist_sq / WIDTH_SQ)
    return jnp.sum(weight[None] * diff, axis=2)


def domain_forces(local):
    atoms = local.shape[1]
    rows = 256
    blocks = local.reshape(3, atoms // rows, rows).transpose(1, 0, 2)
    result = lax.map(lambda block: pair_block(block, local), blocks)
    return result.transpose(1, 0, 2).reshape(3, atoms)


def slot_ids(path_count, path_order, slots):
    offsets = jnp.cumsum(path_count) - path_count
    steps_k = jnp.arange(slots, dtype=jnp.int32)
    live = steps_k[None, :] < path_count[:, None]
    place = jnp.clip(offsets[:, None] + steps_k[None, :], 0, P_SIZE - 1)
    ids = jnp.where(live, path_order[place], -1)
    return (ids, live)


def cv_terms(dist, frame_rank):
    frames_n = dist.shape[0]
    expo = -STRENGTH * dist
    top = jnp.max(expo)
    expd = jnp.exp(expo - top)
    total = jnp.sum(expd)
    weight = expd / total
    progress_rank = frame_rank.astype(jnp.float32) / (frames_n - 1.0)
    s_value = jnp.sum(progress_rank * weight)
    z_value = -(top + jnp.log(total)) / STRENGTH
    grads = (
        KAPPA_S * P_SIZE * (s_value - S_HOME) * -STRENGTH * weight * (progress_rank - s_value)
        + KAPPA_Z * P_SIZE * z_value * weight
    )
    return (s_value, z_value, grads)


def summed_terms(partial_value, frame_rank):
    dist = one_axis_at_a_time(partial_value, GX_GY_GZ)
    return cv_terms(dist, frame_rank)


def body(positions, frames, path_slot, path_count, path_order, frame_rank):
    slots = path_slot.shape[1]
    local_slot = path_slot[0]
    ids, live = slot_ids(path_count, path_order, slots)
    path_pos = jnp.take(positions, local_slot, axis=1)
    here = lax.axis_index(GX_GY_GZ)
    my_ids = lax.dynamic_slice_in_dim(ids, here, 1, 0)[0]
    mask = lax.dynamic_slice_in_dim(live, here, 1, 0)[0].astype(jnp.float32)
    whole = lax.all_gather(frames, GY_GZ, axis=2, tiled=True)
    refs = jnp.take(whole, jnp.clip(my_ids, 0, P_SIZE - 1), axis=2)
    delta = path_pos[None] - refs
    partial_value = jnp.sum(jnp.sum(delta * delta, axis=1) * mask[None], axis=1) / P_SIZE
    s_value, z_value, grads = summed_terms(partial_value, frame_rank)
    bias = (
        -(2.0 / P_SIZE)
        * jnp.einsum("f,fcm->cm", grads, delta, precision=lax.Precision.HIGHEST)
        * mask[None]
    )
    forces = domain_forces(positions)
    forces = forces.at[:, local_slot].add(bias)
    return (forces, jnp.stack([s_value, z_value]))


def solution(mesh):
    finer = Mesh(
        mesh.devices.reshape(mesh.shape["gx"], mesh.shape["gy"], 8, 2), ("gx", "gy", "gz_0", "gz_1")
    )
    return jax.shard_map(
        body,
        mesh=finer,
        in_specs=(P(None, GX_GY_GZ), P(None, None, GY_GZ), P(GX_GY_GZ, None), P(), P(), P()),
        out_specs=(P(None, GX_GY_GZ), P()),
        check_vma=False,
    )
```

profile of v0, /device:TPU:1, one launch (start us, length us, event | category | flops | bytes accessed | tf_op | source)
XLA Modules:
  0.0 190.1 jit_solution(15374449258505947878)
XLA Ops:
  7.2 0.7 all-gather.2.cloned.1.call-update
  7.9 1.0 reduce-window.9
  9.1 0.8 bitcast_subtract_fusion.1
  10.2 90.5 %gather_fusion.1 = s32[16384]{0:T(1024)S(1)} fusion(s32[4096]{0:T(1024)S(1)} %copy-done, s32[16384]{0:T(1024)S(1)} %broadcast_clamp_fusion), kind=kCustom, calls=%fused_computation.1 | custom fusion | bytes 196608 | tf_op jit(solution)/shard_map/gather | solution.py:44
  101.1 1.5 while.10
  101.1 0.2 fusion.25
  101.4 0.4 fusion.26
  101.8 0.2 fusion.25
  102.1 0.4 fusion.26
  102.7 0.6 gather_fusion
  103.6 10.7 %copy.22 = f32[128,3,4096]{0,1,2:T(4,128)} copy(f32[128,3,4096]{0,2,1:T(8,128)} %all-gather.2.cloned.1.call-done) | data formatting | bytes 12582912 | tf_op jit(solution)/shard_map/all_gather | solution.py:78
  114.3 4.0 %gather_fusion.2 = f32[32,128,3]{1,2,0:T(4,128)S(1)} fusion(f32[128,3,4096]{0,1,2:T(4,128)} %copy.22, s32[1024]{0:T(1024)S(1)} %pad_clamp_fusion), kind=kCustom, calls=%fused_computation.2 | custom fusion | bytes 98432 | tf_op jit(solution)/shard_map/jit(_take)/gather | solution.py:79
  118.3 0.1 multiply_reduce_fusion
  118.5 9.3 %psum.28 = f32[128]{0:T(128)S(1)} all-reduce(f32[128]{0:T(128)S(1)} %broadcast_multiply_fusion), channel_id=1, replica_groups=mesh['gx'=4,'gy'=8,'gz_0'=8,'gz_1'=2] {'gx'}, use_global_device_ids=true, to_apply=%region_8.9 | all-reduce | flops 128 | bytes 1024 | tf_op jit(solution)/shard_map/psum | solution.py:20
  127.8 19.5 %psum.29 = f32[128]{0:T(128)S(1)} all-reduce(f32[128]{0:T(128)S(1)} %psum.28), channel_id=1, replica_groups=mesh['gx'=4,'gy'=8,'gz_0'=8,'gz_1'=2] {'gy'}, use_global_device_ids=true, to_apply=%region_9.10 | all-reduce | flops 128 | bytes 1024 | tf_op jit(solution)/shard_map/psum | solution.py:20
  147.3 13.8 %psum.30 = f32[128]{0:T(128)S(1)} all-reduce(f32[128]{0:T(128)S(1)} %psum.29), channel_id=1, replica_groups=mesh['gx'=4,'gy'=8,'gz_0'=8,'gz_1'=2] {'gz_0'}, use_global_device_ids=true, to_apply=%region_10.11 | all-reduce | flops 128 | bytes 1024 | tf_op jit(solution)/shard_map/psum | solution.py:20
  161.1 12.3 %psum.31 = f32[128]{0:T(128)S(1)} all-reduce(f32[128]{0:T(128)S(1)} %psum.30), channel_id=1, replica_groups=mesh['gx'=4,'gy'=8,'gz_0'=8,'gz_1'=2] {'gz_1'}, use_global_device_ids=true, to_apply=%region_11.12 | all-reduce | flops 128 | bytes 1024 | tf_op jit(solution)/shard_map/psum | solution.py:20
  173.4 0.6 multiply_reduce_fusion.3
  174.0 1.3 fusion.21
  176.6 2.0 %multiply_reduce_fusion.2 = (f32[]{:T(128)}, f32[128]{0:T(128)S(1)}) fusion(s32[128]{0:T(128)S(1)} %copy-done.3, f32[]{:T(128)} %fusion.21, f32[]{:T(128)} %multiply_reduce_fusion.3, f32[128]{0:T(128)S(1)} %psum.31), kind=kLoop, calls=%fused_computation.47 | loop fusion | flops 895 | bytes 1548 | tf_op jit(solution)/shard_map/reduce_sum | solution.py:56
  179.3 0.9 fusion.2
  180.3 1.0 scatter_custom_fusion
  181.3 0.7 copy.23
  182.0 1.3 pad_maximum_fusion
  (40 shorter events, 1.7 us)
Async XLA Ops:
  7.2 3.0 %copy-start = (s32[4096]{0:T(1024)S(1)}, s32[4096]{0:T(1024)}, u32[]{:S(2)}) copy-start(s32[4096]{0:T(1024)} %param.12) | copy-start | bytes 49156
  7.2 96.4 %all-gather.2.cloned.1.call-start = ((), (), s32[]{:S(2)}) async-start(), calls=%async_computation | async-start | bytes 6340608 | tf_op jit(solution)/shard_map/all_gather | solution.py:78
  10.2 90.7 %copy-start.1 = (f32[3,512]{1,0:T(4,128)S(1)}, f32[3,512]{1,0:T(4,128)}, u32[]{:S(2)}) copy-start(f32[3,512]{1,0:T(4,128)} %param.8) | copy-start | bytes 18436
  101.0 1.6 copy-start.4
  101.0 2.2 %copy-start.2 = (s32[512]{0:T(512)S(1)}, s32[512]{0:T(512)}, u32[]{:S(2)}) copy-start(s32[512]{0:T(512)} %param.11) | copy-start | bytes 6148
  103.6 73.0 %copy-start.3 = (s32[128]{0:T(128)S(1)}, s32[128]{0:T(128)}, u32[]{:S(2)}) copy-start(s32[128]{0:T(128)} %param.13) | copy-start | bytes 1540
Sparse Core Ops, SparseCore 0:
  11.2 91.8 all-gather.1
where the time goes:
time: 191 us; the launch traced here: 190 us
  local copies, waits for them, and re-layouts  107 us (56%)
  blocking collectives  54.9 us (29%)
  between operations  16.3 us (9%)
  other arithmetic  9.86 us (5%)
    gather x2, local copies, waits for them, and re-layouts, slot_ids(): ids = jnp.where(live, path_order[place], -1)  90.7 us
    psum x4, blocking collectives, one_axis_at_a_time(): array = lax.psum(array, axis)  54.9 us
    all_gather x1, local copies, waits for them, and re-layouts, body(): whole = lax.all_gather(frames, GY_GZ, axis=2, tiled=True)  10.7 us
    gather x1, local copies, waits for them, and re-layouts, body(): refs = jnp.take(whole, jnp.clip(my_ids, 0, P_SIZE - 1), axis=2)  3.99 us
  transfers between devices with their start and end apart: 1, of which 0 were waited for; matrix products, arithmetic and copies ran while one was open for 50% of the time, Pallas kernels for 0%

commit v1 on v0

--- a/solution.py
+++ b/solution.py
@@ -75,7 +75,7 @@
     here = lax.axis_index(GX_GY_GZ)
     my_ids = lax.dynamic_slice_in_dim(ids, here, 1, 0)[0]
     mask = lax.dynamic_slice_in_dim(live, here, 1, 0)[0].astype(jnp.float32)
-    whole = lax.all_gather(frames, GY_GZ, axis=2, tiled=True)
+    whole = jnp.concatenate(lax.all_gather(frames, GY_GZ), axis=2)
     refs = jnp.take(whole, jnp.clip(my_ids, 0, P_SIZE - 1), axis=2)
     delta = path_pos[None] - refs
     partial_value = jnp.sum(jnp.sum(delta * delta, axis=1) * mask[None], axis=1) / P_SIZE

time: 191 us -> 206 us (1.079)
  local copies, waits for them, and re-layouts: 107 us -> 123 us
  blocking collectives: 54.9 us -> 52.8 us
  waiting for transfers between devices: 0.68 us -> 2.77 us
    reshape x0 -> x2, local copies, waits for them, and re-layouts: none -> 22.3 us  [body(): whole = jnp.concatenate(lax.all_gather(frames, GY_GZ), axis=2)]
    all_gather x1 -> x0, local copies, waits for them, and re-layouts: 10.7 us -> none  [body(): whole = lax.all_gather(frames, GY_GZ, axis=2, tiled=True)]
    unnamed x12 -> x13, local copies, waits for them, and re-layouts: 0.89 us -> 4.76 us
    all_gather x1, waiting for transfers between devices: 0.01 us -> 2.09 us  [body(): whole = jnp.concatenate(lax.all_gather(frames, GY_GZ), axis=2)]
    psum x4, blocking collectives: 54.9 us -> 52.8 us  [one_axis_at_a_time(): array = lax.psum(array, axis)]
  transfers between devices with their start and end apart: 1 -> 1, of which waited for: 0 -> 1; matrix products, arithmetic and copies ran while one was open for 50% -> 46% of each run, Pallas kernels for 0% -> 0%
where the time goes in v1:
time: 206 us
  local copies, waits for them, and re-layouts  123 us (60%)
  blocking collectives  52.8 us (26%)
  between operations  16.3 us (8%)
  other arithmetic  9.86 us (5%)
  waiting for transfers between devices  2.77 us (1%)
    gather x2, local copies, waits for them, and re-layouts, slot_ids(): ids = jnp.where(live, path_order[place], -1)  90.7 us
    psum x4, blocking collectives, one_axis_at_a_time(): array = lax.psum(array, axis)  52.8 us
    reshape x2, local copies, waits for them, and re-layouts, body(): whole = jnp.concatenate(lax.all_gather(frames, GY_GZ), axis=2)  22.3 us
    unnamed x13, local copies, waits for them, and re-layouts  4.76 us
  transfers between devices with their start and end apart: 1, of which 1 were waited for; matrix products, arithmetic and copies ran while one was open for 46% of the time, Pallas kernels for 0%

profile of v1, /device:TPU:1, one launch (start us, length us, event | category | flops | bytes accessed | tf_op | source)
XLA Modules:
  0.0 205.6 jit_solution(1242888163513133791)
XLA Ops:
  7.2 0.7 all-gather.3.cloned.1.call-update
  7.9 1.0 reduce-window.9
  9.1 0.8 bitcast_subtract_fusion.1
  10.2 90.5 %gather_fusion.1 = s32[16384]{0:T(1024)S(1)} fusion(s32[4096]{0:T(1024)S(1)} %copy-done, s32[16384]{0:T(1024)S(1)} %broadcast_clamp_fusion), kind=kCustom, calls=%fused_computation.1 | custom fusion | bytes 196608 | tf_op jit(solution)/shard_map/gather | solution.py:44
  101.1 1.4 while.10
  101.4 0.4 fusion.26
  102.1 0.4 fusion.26
  102.7 0.6 gather_fusion
  103.6 2.1 %all-gather.3.cloned.1.call-done = f32[16384,3,32]{0,2,1:T(8,128)} async-done(((f32[128,3,32]{0,2,1:T(8,128)}), f32[16384,3,32]{0,2,1:T(8,128)}) %all-gather.3.cloned.1.call-update) | async-done | bytes 6291472 | tf_op jit(solution)/shard_map/all_gather | solution.py:78
  105.7 3.9 %copy.33 = f32[12,8,128,128]{3,2,1,0:T(8,128)S(1)} copy(f32[12,8,128,128]{3,1,2,0:T(8,128)} %bitcast.63) | data formatting | bytes 12582912
  109.6 3.6 %copy.28 = f32[128,3,128,32]{0,3,2,1:T(8,128)S(1)} copy(f32[128,3,128,32]{0,2,3,1:T(8,128)S(1)} %bitcast.61) | data formatting | bytes 12582912 | tf_op jit(solution)/shard_map/reshape | solution.py:78
  113.2 18.7 %copy.29 = f32[128,3,4096]{0,1,2:T(4,128)} copy(f32[128,3,4096]{0,2,1:T(8,128)S(1)} %bitcast.62) | data formatting | bytes 12582912 | tf_op jit(solution)/shard_map/reshape | solution.py:78
  131.9 4.0 %gather_fusion.2 = f32[32,128,3]{1,2,0:T(4,128)S(1)} fusion(f32[128,3,4096]{0,1,2:T(4,128)} %copy.29, s32[1024]{0:T(1024)S(1)} %pad_clamp_fusion), kind=kCustom, calls=%fused_computation.2 | custom fusion | bytes 98432 | tf_op jit(solution)/shard_map/jit(_take)/gather | solution.py:79
  136.1 8.3 %psum.28 = f32[128]{0:T(128)S(1)} all-reduce(f32[128]{0:T(128)S(1)} %broadcast_multiply_fusion), channel_id=1, replica_groups=mesh['gx'=4,'gy'=8,'gz_0'=8,'gz_1'=2] {'gx'}, use_global_device_ids=true, to_apply=%region_8.9 | all-reduce | flops 128 | bytes 1024 | tf_op jit(solution)/shard_map/psum | solution.py:20
  144.4 18.4 %psum.29 = f32[128]{0:T(128)S(1)} all-reduce(f32[128]{0:T(128)S(1)} %psum.28), channel_id=1, replica_groups=mesh['gx'=4,'gy'=8,'gz_0'=8,'gz_1'=2] {'gy'}, use_global_device_ids=true, to_apply=%region_9.10 | all-reduce | flops 128 | bytes 1024 | tf_op jit(solution)/shard_map/psum | solution.py:20
  162.8 13.8 %psum.30 = f32[128]{0:T(128)S(1)} all-reduce(f32[128]{0:T(128)S(1)} %psum.29), channel_id=1, replica_groups=mesh['gx'=4,'gy'=8,'gz_0'=8,'gz_1'=2] {'gz_0'}, use_global_device_ids=true, to_apply=%region_10.11 | all-reduce | flops 128 | bytes 1024 | tf_op jit(solution)/shard_map/psum | solution.py:20
  176.6 12.3 %psum.31 = f32[128]{0:T(128)S(1)} all-reduce(f32[128]{0:T(128)S(1)} %psum.30), channel_id=1, replica_groups=mesh['gx'=4,'gy'=8,'gz_0'=8,'gz_1'=2] {'gz_1'}, use_global_device_ids=true, to_apply=%region_11.12 | all-reduce | flops 128 | bytes 1024 | tf_op jit(solution)/shard_map/psum | solution.py:20
  188.9 0.6 multiply_reduce_fusion.3
  189.5 1.3 fusion.21
  192.1 2.0 multiply_reduce_fusion.2
  194.8 0.9 fusion.2
  195.8 1.0 scatter_custom_fusion
  196.8 0.7 copy.30
  197.5 1.3 pad_maximum_fusion
  (42 shorter events, 2.2 us)
Async XLA Ops:
  7.2 3.0 %copy-start = (s32[4096]{0:T(1024)S(1)}, s32[4096]{0:T(1024)}, u32[]{:S(2)}) copy-start(s32[4096]{0:T(1024)} %param.12) | copy-start | bytes 49156
  7.2 98.5 %all-gather.3.cloned.1.call-start = ((), (), s32[]{:S(2)}) async-start(), calls=%async_computation | async-start | bytes 6340608 | tf_op jit(solution)/shard_map/all_gather | solution.py:78
  10.2 90.7 %copy-start.1 = (f32[3,512]{1,0:T(4,128)S(1)}, f32[3,512]{1,0:T(4,128)}, u32[]{:S(2)}) copy-start(f32[3,512]{1,0:T(4,128)} %param.8) | copy-start | bytes 18436
  101.0 1.6 copy-start.4
  101.0 2.2 %copy-start.2 = (s32[512]{0:T(512)S(1)}, s32[512]{0:T(512)}, u32[]{:S(2)}) copy-start(s32[512]{0:T(512)} %param.11) | copy-start | bytes 6148
  113.2 78.9 %copy-start.3 = (s32[128]{0:T(128)S(1)}, s32[128]{0:T(128)}, u32[]{:S(2)}) copy-start(s32[128]{0:T(128)} %param.13) | copy-start | bytes 1540
Sparse Core Ops, SparseCore 0:
  11.0 94.6 all-gather.2
